TPU v7x, 32 devices: a whole 2x2x4 slice. The times are simulated.
32 devices in a mesh: freq: 4 (over y, x), shot: 8 (over z, core).
Axes of the slice: x: 2, y: 2, z: 4, core: 2. Of those that a mesh axis runs over, the one named last changes fastest.
Arguments:
- traces: bfloat16 [2, 4, 3072, 3072], P(None, 'freq', 'shot'), may hold values from -40 to 40, as said below
Outputs:
- multiples: bfloat16 [2, 4, 3072, 3072], P(None, 'freq', 'shot')
- primaries: bfloat16 [2, 4, 3072, 3072], P(None, 'freq', 'shot')
Inputs may be any that keep to these rules, and one draw needn't show every extreme that they name: `traces`: finite recorded data.
All inputs are finite; a program needn't handle non-finite values.
Results may differ from a plain program's by a relative error of at most 0.0005.
Values may be sent and summed in bfloat16 or wider, within the bound.
A program may use at most 192 MiB of HBM per device.

v0:
```python
import math

import jax
import jax.numpy as jnp
from jax import lax
from jax.sharding import PartitionSpec as P

epsilon = 1e-06


def complex_product(left_re, left_im, right):
    left_block = jnp.stack(
        [jnp.concatenate([left_re, -left_im], axis=2), jnp.concatenate([left_im, left_re], axis=2)]
    )
    right_block = jnp.concatenate([right[0], right[1]], axis=1)
    return jnp.einsum("cfik,fkn->cfin", left_block, right_block, preferred_element_type=jnp.float32)


def per_device(traces):
    matrix_order = traces.shape[3]
    bands = traces.shape[1]
    factor = 1.0 / math.sqrt(matrix_order)
    real_part = traces[0]
    imag_part = traces[1]
    products = complex_product(
        real_part, imag_part, lax.all_gather(traces, "shot", axis=2, tiled=True)
    )
    mult_re = products[0] * factor
    mult_im = products[1] * factor
    data_re = traces[0].astype(jnp.float32)
    data_im = traces[1].astype(jnp.float32)
    partial_sums = (
        jnp.sum(mult_re * data_re + mult_im * data_im),
        jnp.sum(mult_re * data_im - mult_im * data_re),
        jnp.sum(mult_re * mult_re + mult_im * mult_im),
    )
    group_sums = lax.psum((partial_sums[0], partial_sums[1], partial_sums[2]), "shot")
    num_re, num_im, denom = lax.psum((group_sums[0], group_sums[1], group_sums[2]), "freq")
    total_count = float(bands * lax.axis_size("freq") * matrix_order * matrix_order)
    scaled_den = denom / total_count + epsilon
    fit_re = num_re / total_count / scaled_den
    fit_im = num_im / total_count / scaled_den
    prim_re = data_re - (fit_re * mult_re - fit_im * mult_im)
    prim_im = data_im - (fit_re * mult_im + fit_im * mult_re)
    multiples = jnp.stack([mult_re, mult_im]).astype(jnp.bfloat16)
    primaries = jnp.stack([prim_re, prim_im]).astype(jnp.bfloat16)
    return (multiples, primaries)


def solution(mesh):
    placed = (P(None, "freq", "shot", None),)
    return jax.shard_map(
        per_device,
        mesh=mesh,
        in_specs=placed,
        out_specs=(P(None, "freq", "shot", None), P(None, "freq", "shot", None)),
        check_vma=False,
    )
```

profile of v0, /device:TPU:0, one launch (start us, length us, event | category | flops | bytes accessed | tf_op | source)
XLA Modules:
  0.0 455.3 jit_solution(17168837838430038316)
XLA Ops:
  7.2 0.0 all-gather.2.cloned.1.call-start
  7.2 6.7 %copy.3 = bf16[2,1,384,3072]{2,3,1,0:T(8,128)(2,1)} copy(bf16[2,1,384,3072]{3,2,1,0:T(8,128)(2,1)} %param.1) | data formatting | bytes 9437184 | tf_op args[0]
  13.9 0.0 all-gather.2.cloned.1.call-update
  13.9 1.8 fusion.15
  15.7 2.7 slice_bitcast_fusion.2
  18.4 3.9 maximum_bitcast_fusion.8
  22.3 318.7 %all-gather.2.cloned.1.call-done = bf16[2,1,3072,3072]{2,3,1,0:T(8,128)(2,1)} async-done(((bf16[2,1,384,3072]{2,3,1,0:T(8,128)(2,1)}), bf16[2,1,3072,3072]{2,3,1,0:T(8,128)(2,1)}) %all-gather.2.cloned.1.call-update) | async-done | bytes 37748752 | tf_op jit(solution)/shard_map/all_gather | solution.py:26
  341.0 25.2 %slice_bitcast_fusion.1 = (bf16[1,3072,3072]{1,2,0:T(8,128)(2,1)}, bf16[1,3072,3072]{1,2,0:T(8,128)(2,1)}) fusion(bf16[2,1,3072,3072]{2,3,1,0:T(8,128)(2,1)} %all-gather.2.cloned.1.call-done), kind=kLoop, calls=%fused_computation.5 | loop fusion | bytes 75497472 | tf_op jit(solution)/shard_map/squeeze | solution.py:15
  366.2 37.2 %fusion.5 = f32[2,1,384,3072]{3,2,1,0:T(8,128)} fusion(bf16[1,1,384,6144]{3,2,0,1:T(8,128)(2,1)} %get-tuple-element.20, bf16[1,1,384,6144]{3,2,0,1:T(8,128)(2,1)} %get-tuple-element.19, bf16[1,3072,3072]{1,2,0:T(8,128)(2,1)} %get-tuple-element.12, bf16[1,3072,3072]{1,2,0:T(8,128)(2,1)} %get-tuple-element.11), kind=kOutput, calls=%fused_computation.13 | convolution fusion | flops 29085401088 | bytes 56623104 | tf_op jit(solution)/shard_map/cfik,fkn->cfin/dot_general | solution.py:16
  403.4 6.9 %fusion.7 = (f32[]{:T(128)}, f32[]{:T(128)}, f32[]{:T(128)}) fusion(f32[2,1,384,3072]{3,2,1,0:T(8,128)} %fusion.5, bf16[2,1,384,3072]{3,2,1,0:T(8,128)(2,1)} %param.1), kind=kLoop, calls=%fused_computation.15 | loop fusion | flops 18874364 | bytes 14155788 | tf_op jit(solution)/shard_map/reduce_sum | solution.py:33
  410.4 15.0 %all-reduce = (f32[]{:T(128)}, f32[]{:T(128)}, f32[]{:T(128)}) all-reduce(f32[]{:T(128)} %get-tuple-element.3, f32[]{:T(128)} %get-tuple-element.4, f32[]{:T(128)} %get-tuple-element.2), channel_id=1, replica_groups=mesh['freq'=4,'shot'=8] {'shot'}, use_global_device_ids=true, to_apply=%region_7.0 | all-reduce | flops 3 | bytes 24 | tf_op jit(solution)/shard_map/psum | solution.py:37
  425.4 10.7 %all-reduce.1 = (f32[]{:T(128)}, f32[]{:T(128)}, f32[]{:T(128)}) all-reduce(f32[]{:T(128)} %get-tuple-element.5, f32[]{:T(128)} %get-tuple-element.6, f32[]{:T(128)} %get-tuple-element.7), channel_id=1, replica_groups=mesh['freq'=4,'shot'=8] {'freq'}, use_global_device_ids=true, to_apply=%region_8.0 | all-reduce | flops 3 | bytes 24 | tf_op jit(solution)/shard_map/psum | solution.py:38
  438.2 6.3 %subtract_convert_fusion.1 = (bf16[1,1,384,3072]{3,2,1,0:T(8,128)(2,1)S(1)}, bf16[1,1,384,3072]{3,2,1,0:T(8,128)(2,1)S(1)}, bf16[1,1,384,3072]{3,2,1,0:T(8,128)(2,1)S(1)}, bf16[1,1,384,3072]{3,2,1,0:T(8,128)(2,1)S(1)}) fusion(f32[2,1,384,3072]{3,2,1,0:T(8,128)} %fusion.5, f32[]{:T(128)S(6)} %mul.163, f32[]{:T(128)S(6)} %mul.158, ...), kind=kLoop, calls=%fused_computation.27 | loop fusion | flops 18874368 | bytes 23592968 | tf_op jit(solution)/shard_map/convert
  444.5 3.9 pad_maximum_fusion
Async XLA Ops:
  7.2 333.8 %all-gather.2.cloned.1.call-start = ((), (), s32[]{:S(2)}) async-start(), calls=%async_computation | async-start | bytes 42467328 | tf_op jit(solution)/shard_map/all_gather | solution.py:26
Sparse Core Ops, SparseCore 0:
  14.0 326.9 all-gather.1
where the time goes:
time: 456 us; the launch traced here: 455 us
  waiting for transfers between devices  319 us (70%)
  matrix products  37.2 us (8%)
  local copies, waits for them, and re-layouts  34.6 us (8%)
  blocking collectives  25.8 us (6%)
  other arithmetic  22.9 us (5%)
  between operations  16.1 us (4%)
    all_gather x1, waiting for transfers between devices, per_device(): lax.all_gather(traces, 'shot', axis=2, tiled=True)  319 us
    dot_general x1, matrix products, complex_product(): jnp.einsum('cfik,fkn->cfin', left_block, right_block, preferred_element_t...  37.2 us
    squeeze x1, local copies, waits for them, and re-layouts, complex_product(): right_block = jnp.concatenate([right[0], right[1]], axis=1)  25.2 us
    psum x1, blocking collectives, per_device(): lax.psum((partial_sums[0], partial_sums[1], partial_sums[2]), 'shot')  15 us
    psum x1, blocking collectives, per_device(): lax.psum((group_sums[0], group_sums[1], group_sums[2]), 'freq')  10.7 us
  transfers between devices with their start and end apart: 1, of which 1 were waited for; matrix products, arithmetic and copies ran while one was open for 2% of the time, Pallas kernels for 0%

commit v1 on v0

v1 whole, which is shorter than its diff:
```python
import functools
import math

import jax
import jax.numpy as jnp
from jax import lax
from jax.experimental import pallas as pl
from jax.experimental.pallas import tpu as pltpu
from jax.sharding import PartitionSpec as P

epsilon = 1e-06
MESH = pl.DeviceIdType.MESH


def complex_product(left_re, left_im, right):
    left_block = jnp.stack(
        [jnp.concatenate([left_re, -left_im], axis=2), jnp.concatenate([left_im, left_re], axis=2)]
    )
    right_block = jnp.concatenate([right[0], right[1]], axis=1)
    return jnp.einsum("cfik,fkn->cfin", left_block, right_block, preferred_element_type=jnp.float32)


def finish(traces, mult_re, mult_im, num_re, num_im, denom):
    matrix_order = traces.shape[3]
    data_re = traces[0].astype(jnp.float32)
    data_im = traces[1].astype(jnp.float32)
    total_count = float(traces.shape[1] * lax.axis_size("freq") * matrix_order * matrix_order)
    scaled_den = denom / total_count + epsilon
    fit_re = num_re / total_count / scaled_den
    fit_im = num_im / total_count / scaled_den
    prim_re = data_re - (fit_re * mult_re - fit_im * mult_im)
    prim_im = data_im - (fit_re * mult_im + fit_im * mult_re)
    multiples = jnp.stack([mult_re, mult_im]).astype(jnp.bfloat16)
    primaries = jnp.stack([prim_re, prim_im]).astype(jnp.bfloat16)
    return (multiples, primaries)


def gathered(traces):
    factor = 1.0 / math.sqrt(traces.shape[3])
    products = complex_product(
        traces[0], traces[1], lax.all_gather(traces, "shot", axis=2, tiled=True)
    )
    mult_re = products[0] * factor
    mult_im = products[1] * factor
    data_re = traces[0].astype(jnp.float32)
    data_im = traces[1].astype(jnp.float32)
    sums = lax.psum(
        jnp.stack([
            jnp.sum(mult_re * data_re + mult_im * data_im),
            jnp.sum(mult_re * data_im - mult_im * data_re),
            jnp.sum(mult_re * mult_re + mult_im * mult_im),
        ]),
        ("freq", "shot"),
    )
    return finish(traces, mult_re, mult_im, sums[0], sums[1], sums[2])


def line_kernel(
    chunks, kept, width, step, freqs, shots,
    traces_ref, mult_ref, total_ref,
    grid, own_stage, help_stage, acc, sums,
    load_sem, out_sem, ici_recv, pair_recv, far_send, end_send, pair_send,
    result_send, result_recv, sum_send, sum_recv,
):
    rows = traces_ref.shape[1]
    order = traces_ref.shape[2]
    factor = 1.0 / math.sqrt(order)
    freq = lax.axis_index("freq")
    shot = lax.axis_index("shot")
    z = shot // 2
    core = shot % 2
    low = z < 2
    end = jnp.where(low, 0, 3)
    mid = jnp.where(low, 1, 2)
    far_mid = jnp.where(low, 2, 1)
    far_end = jnp.where(low, 3, 0)
    is_end = z == end

    def block(chip, plane, j):
        first = pl.multiple_of((chip * 2 + plane) * rows, rows)
        return grid.at[:, pl.ds(first, rows), pl.ds(pl.multiple_of(j * width, width), width)]

    def remote(src, dst, send, recv, chip, plane):
        return pltpu.make_async_remote_copy(
            src_ref=src, dst_ref=dst, send_sem=send, recv_sem=recv,
            device_id=(freq, chip * 2 + plane), device_id_type=MESH,
        )

    def ici(chip, j, send, slot, target):
        ref = block(chip, core, j)
        return remote(ref, ref, send, ici_recv.at[slot, j], target, core)

    def pair(chip, j, slot):
        ref = block(chip, core, j)
        return remote(ref, ref, pair_send.at[slot, j], pair_recv.at[slot, j], z, 1 - core)

    def arrived(chip, j, slot):
        ref = block(chip, core, j)
        remote(ref, ref, far_send.at[0, j], ici_recv.at[slot, j], z, 1 - core).wait_recv()

    def paired(chip, j, slot):
        ref = block(chip, 1 - core, j)
        remote(ref, ref, pair_send.at[slot, j], pair_recv.at[slot, j], z, 1 - core).wait_recv()

    def to_end(chip, j, slot):
        return ici(chip, j, end_send.at[slot, j], slot, end)

    def to_far(chip, j, slot):
        return ici(chip, j, far_send.at[slot, j], slot + 1, far_mid)

    def to_mid(j):
        return ici(z, j, end_send.at[0, j], 0, mid)

    def own_out(j, s):
        return pltpu.make_async_copy(
            own_stage.at[s],
            mult_ref.at[:, :, pl.ds(pl.multiple_of(j * width, width), width)],
            out_sem.at[s],
        )

    def result(j, s):
        return remote(
            help_stage.at[s],
            mult_ref.at[:, :, pl.ds(pl.multiple_of(j * width, width), width)],
            result_send.at[s], result_recv.at[j], end, core,
        )

    def multiply(chip, j, stage, s):
        first = pl.multiple_of((chip * 2 + core) * rows, rows)

        def part(q, carry):
            column = pl.multiple_of(j * width + q * step, step)
            left_re = grid[0, pl.ds(first, rows), :]
            left_im = grid[1, pl.ds(first, rows), :]
            right_re = grid[0, :, pl.ds(column, step)]
            right_im = grid[1, :, pl.ds(column, step)]
            dot = functools.partial(jnp.dot, preferred_element_type=jnp.float32)
            mult_re = (dot(left_re, right_re) - dot(left_im, right_im)) * factor
            mult_im = (dot(left_re, right_im) + dot(left_im, right_re)) * factor
            here = pl.ds(pl.multiple_of(q * step, step), step)
            stage[s, 0, :, here] = mult_re
            stage[s, 1, :, here] = mult_im
            data_re = grid[0, pl.ds(first, rows), pl.ds(column, step)].astype(jnp.float32)
            data_im = grid[1, pl.ds(first, rows), pl.ds(column, step)].astype(jnp.float32)
            for i, term in enumerate((
                mult_re * data_re + mult_im * data_im,
                mult_re * data_im - mult_im * data_re,
                mult_re * mult_re + mult_im * mult_im,
            )):
                folded = jnp.sum(term.reshape(rows // 8, 8, step), axis=0)
                lanes = folded[:, :128]
                for k in range(1, step // 128):
                    lanes = lanes + folded[:, k * 128:(k + 1) * 128]
                acc[pl.ds(i * 8, 8), :] += lanes
            return carry

        lax.fori_loop(0, width // step, part, 0)

    acc[...] = jnp.zeros_like(acc)
    mine = grid.at[:, pl.ds(pl.multiple_of(shot * rows, rows), rows), :]
    load = pltpu.make_async_copy(traces_ref, mine, load_sem)
    load.start()
    load.wait()

    def loop(lower, upper, body):
        def run(j, carry):
            body(j)
            return carry
        lax.fori_loop(lower, upper, run, 0)

    @pl.when(is_end)
    def _():
        def first_sends(j):
            to_mid(j).start()

            @pl.when(j < kept)
            def _():
                pair(z, j, 3).start()

        loop(0, chunks, first_sends)

        def work(j):
            for slot, chip in enumerate((mid, far_mid, far_end)):
                arrived(chip, j, slot)
                pair(chip, j, slot).start()
            for slot, chip in enumerate((mid, far_mid, far_end, end)):
                paired(chip, j, slot)
            s = j % 2

            @pl.when(j >= 2)
            def _():
                own_out(j - 2, s).wait()
            multiply(z, j, own_stage, s)
            own_out(j, s).start()

        loop(0, kept, work)
        loop(kept - 2, kept, lambda j: own_out(j, j % 2).wait())

        def drain(j):
            to_mid(j).wait_send()

            @pl.when(j < kept)
            def _():
                for slot, chip in enumerate((mid, far_mid, far_end, end)):
                    pair(chip, j, slot).wait_send()

        loop(0, chunks, drain)

    @pl.when(jnp.logical_not(is_end))
    def _():
        def own_sends(j):
            to_far(z, j, 0).start()

            @pl.when(j < kept)
            def _():
                to_end(z, j, 0).start()
            pair(z, j, 3).start()

        def near(j):
            arrived(end, j, 0)
            to_far(end, j, 1).start()
            pair(end, j, 0).start()

        ahead = 2
        loop(0, ahead, own_sends)
        loop(0, ahead, near)

        def work(j):
            upper = jnp.where(j < kept, jnp.minimum(j + ahead + 1, chunks), chunks)
            lower = jnp.where(j <= kept, jnp.minimum(j + ahead, chunks), chunks)

            def more(jj):
                own_sends(jj)
                near(jj)

            loop(lower, upper, more)
            for slot, chip in ((1, far_mid), (2, far_end)):
                arrived(chip, j, slot)

                @pl.when(j < kept)
                def _():
                    to_end(chip, j, slot).start()
                pair(chip, j, slot).start()
            for slot, chip in enumerate((end, far_mid, far_end, z)):
                paired(chip, j, slot)
            s = j % 2

            @pl.when(j >= kept)
            def _():
                @pl.when(j >= kept + 2)
                def _():
                    result(j - 2, s).wait_send()
                multiply(end, j, help_stage, s)
                result(j, s).start()

            @pl.when(j >= 2)
            def _():
                own_out(j - 2, s).wait()
            multiply(z, j, own_stage, s)
            own_out(j, s).start()

        loop(0, chunks, work)

        def drain(j):
            to_far(z, j, 0).wait_send()
            to_far(end, j, 1).wait_send()
            for slot, chip in enumerate((end, far_mid, far_end, z)):
                pair(chip, j, slot).wait_send()

            @pl.when(j < kept)
            def _():
                for slot, chip in enumerate((z, far_mid, far_end)):
                    to_end(chip, j, slot).wait_send()

        loop(0, chunks, drain)

    devices = freqs * shots
    me = freq * shots + shot

    def give(d):
        target = (me + d) % devices
        return pltpu.make_async_remote_copy(
            src_ref=acc, dst_ref=sums.at[d - 1],
            send_sem=sum_send.at[d - 1], recv_sem=sum_recv.at[d - 1],
            device_id=(target // shots, target % shots), device_id_type=MESH,
        )

    loop(1, devices, lambda d: give(d).start())
    loop(1, devices, lambda d: give(d).wait_recv())
    total_ref[...] = acc[...] + jnp.sum(sums[...], axis=0)

    @pl.when(is_end)
    def _():
        loop(kept, chunks, lambda j: result(j, 0).wait_recv())

    @pl.when(jnp.logical_not(is_end))
    def _():
        def last(j):
            own_out(j, j % 2).wait()
            result(j, j % 2).wait_send()
        loop(chunks - 2, chunks, last)

    loop(1, devices, lambda d: give(d).wait_send())


def on_a_line(traces):
    rows, order = traces.shape[2], traces.shape[3]
    freqs, shots = lax.axis_size("freq"), lax.axis_size("shot")
    step = 256
    width = step
    chunks = order // width
    kept = chunks // 3
    devices = freqs * shots
    dma = pltpu.SemaphoreType.DMA
    mult, totals = pl.pallas_call(
        functools.partial(line_kernel, chunks, kept, width, step, freqs, shots),
        out_shape=(
            jax.ShapeDtypeStruct((2, rows, order), jnp.float32),
            jax.ShapeDtypeStruct((24, 128), jnp.float32),
        ),
        in_specs=[pl.BlockSpec(memory_space=pl.ANY)],
        out_specs=(
            pl.BlockSpec(memory_space=pl.ANY),
            pl.BlockSpec(memory_space=pltpu.VMEM),
        ),
        scratch_shapes=[
            pltpu.VMEM((2, order, order), jnp.bfloat16),
            pltpu.VMEM((2, 2, rows, width), jnp.float32),
            pltpu.VMEM((2, 2, rows, width), jnp.float32),
            pltpu.VMEM((24, 128), jnp.float32),
            pltpu.VMEM((devices - 1, 24, 128), jnp.float32),
            dma, dma((2,)), dma((3, chunks)), dma((4, chunks)), dma((2, chunks)),
            dma((3, chunks)), dma((4, chunks)),
            dma((2,)), dma((chunks,)), dma((devices - 1,)), dma((devices - 1,)),
        ],
        compiler_params=pltpu.CompilerParams(
            has_side_effects=True, vmem_limit_bytes=60 * 1024 * 1024
        ),
    )(traces[:, 0])
    sums = jnp.sum(totals.reshape(3, 8 * 128), axis=1)
    return finish(traces, mult[0][None], mult[1][None], sums[0], sums[1], sums[2])


def solution(mesh):
    placed = P(None, "freq", "shot", None)

    def per_device(traces):
        four_chips = mesh.shape["shot"] == 2 * 4
        if four_chips and traces.shape[1] == 1 and traces.shape[3] % 256 == 0:
            return on_a_line(traces)
        return gathered(traces)

    return jax.shard_map(
        per_device, mesh=mesh, in_specs=(placed,), out_specs=(placed, placed), check_vma=False
    )
```

time: 456 us -> 282 us (0.62)
  waiting for transfers between devices: 319 us -> 0 us
  Pallas kernels: 0 us -> 265 us
  matrix products: 37.2 us -> 0 us
  local copies, waits for them, and re-layouts: 34.6 us -> 3.11 us
  blocking collectives: 25.8 us -> 0 us
  between operations: 16.1 us -> 2.67 us
  other arithmetic: 22.9 us -> 11 us
    all_gather x1 -> x0, waiting for transfers between devices: 319 us -> none  [per_device(): lax.all_gather(traces, 'shot', axis=2, tiled=True)]
    pallas_call x0 -> x1, Pallas kernels: none -> 265 us  [on_a_line(): pl.pallas_call(functools.partial(line_kernel, chunks, kept, width, step,...]
    dot_general x1 -> x0, matrix products: 37.2 us -> none  [complex_product(): jnp.einsum('cfik,fkn->cfin', left_block, right_block, preferred_element_t...]
    squeeze x2 -> x0, local copies, waits for them, and re-layouts: 27.9 us -> none  [the longest x1 25.2 us: complex_product(): right_block = jnp.concatenate([right[0], right[1]], axis=1)]
    psum x2 -> x0, blocking collectives: 25.8 us -> none  [the longest x1 15 us: per_device(): lax.psum((partial_sums[0], partial_sums[1], partial_sums[2]), 'shot')]
    reduce_sum x1 -> x2, other arithmetic: 6.95 us -> 0.94 us  [on_a_line(): sums = jnp.sum(totals.reshape(3, 8 * 128), axis=1)]
    unnamed x1 -> x2, local copies, waits for them, and re-layouts: 6.66 us -> 1.67 us
    another operation x3 -> x2, other arithmetic: 14.1 us -> 10 us  [the longest x1 6.1 us: finish(): primaries = jnp.stack([prim_re, prim_im]).astype(jnp.bfloat16)]
  transfers between devices with their start and end apart: 1 -> 0, of which waited for: 1 -> 0; matrix products, arithmetic and copies ran while one was open for 2% -> 0% of each run, Pallas kernels for 0% -> 0%
where the time goes in v1:
time: 282 us
  Pallas kernels  265 us (94%)
  other arithmetic  11 us (4%)
  local copies, waits for them, and re-layouts  3.11 us (1%)
    pallas_call x1, Pallas kernels, on_a_line(): pl.pallas_call(functools.partial(line_kernel, chunks, kept, width, step,...  265 us
    another operation x1, other arithmetic, finish(): primaries = jnp.stack([prim_re, prim_im]).astype(jnp.bfloat16)  6.1 us

profile of v1, /device:TPU:0, one launch (start us, length us, event | category | flops | bytes accessed | tf_op | source)
XLA Modules:
  0.0 281.8 jit_solution(3097717127349895217)
XLA Ops:
  0.6 265.0 %shard_map.30 = (f32[2,384,3072]{2,1,0:T(8,128)}, f32[24,128]{1,0:T(8,128)}) custom-call(bf16[2,384,3072]{2,1,0:T(8,128)(2,1)} %bitcast.17), custom_call_target="tpu_custom_call" | custom-call | tf_op jit(solution)/shard_map/pallas_call | solution.py:315
  265.6 0.8 reduce_sum.10
  266.5 0.1 reduce_sum.14
  266.5 0.1 reduce_sum.18
  266.7 0.6 fusion.6
  269.3 0.0 copy-start
  269.3 6.1 %fusion.4 = (bf16[1,1,384,3072]{3,2,1,0:T(8,128)(2,1)S(1)}, bf16[1,1,384,3072]{3,2,1,0:T(8,128)(2,1)S(1)}) fusion(f32[2,384,3072]{2,1,0:T(8,128)} %get-tuple-element.4, f32[]{:T(128)} %bitcast.5, f32[]{:T(128)} %bitcast.4, bf16[2,1,384,3072]{3,2,1,0:T(8,128)(2,1)} %param.1), kind=kLoop, calls=%fused_computation.10 | loop fusion | flops 14155776 | bytes 18874376 | tf_op jit(solution)/shard_map/stack | solution.py:34
  275.4 1.7 copy-done
  277.1 0.7 fusion.2
  277.8 3.9 %pad_maximum_fusion = (bf16[2,1,384,3072]{3,2,1,0:T(8,128)(2,1)}, bf16[2,1,384,3072]{3,2,1,0:T(8,128)(2,1)}) fusion(bf16[1,1,384,3072]{3,2,1,0:T(8,128)(2,1)S(1)} %get-tuple-element.9, bf16[1,1,384,3072]{3,2,1,0:T(8,128)(2,1)S(1)} %get-tuple-element.8, bf16[1,1,384,3072]{3,2,1,0:T(8,128)(2,1)S(1)} %get-tuple-element.7, ...), kind=kLoop, calls=%fused_computation | loop fusion | flops 4718592 | bytes 18874368 | tf_op jit(solution)/shard_map/stack | solution.py:33
Async XLA Ops:
  269.3 7.8 %copy-start = (f32[2,384,3072]{2,1,0:T(8,128)S(1)}, f32[2,384,3072]{2,1,0:T(8,128)}, u32[]{:S(2)}) copy-start(f32[2,384,3072]{2,1,0:T(8,128)} %get-tuple-element.4) | copy-start | bytes 28311556

commit v2 on v1

--- a/solution.py
+++ b/solution.py
@@ -58,12 +58,12 @@
 def line_kernel(
     chunks, kept, width, step, freqs, shots,
     traces_ref, mult_ref, total_ref,
-    grid, own_stage, help_stage, acc, sums,
-    load_sem, out_sem, ici_recv, pair_recv, far_send, end_send, pair_send,
+    grid, help_stage, acc, sums,
+    load_sem, ici_recv, pair_recv, far_send, end_send, pair_send,
     result_send, result_recv, sum_send, sum_recv,
 ):
-    rows = traces_ref.shape[1]
-    order = traces_ref.shape[2]
+    rows = traces_ref.shape[2]
+    order = traces_ref.shape[3]
     factor = 1.0 / math.sqrt(order)
     freq = lax.axis_index("freq")
     shot = lax.axis_index("shot")
@@ -111,13 +111,6 @@
     def to_mid(j):
         return ici(z, j, end_send.at[0, j], 0, mid)
 
-    def own_out(j, s):
-        return pltpu.make_async_copy(
-            own_stage.at[s],
-            mult_ref.at[:, :, pl.ds(pl.multiple_of(j * width, width), width)],
-            out_sem.at[s],
-        )
-
     def result(j, s):
         return remote(
             help_stage.at[s],
@@ -125,7 +118,7 @@
             result_send.at[s], result_recv.at[j], end, core,
         )
 
-    def multiply(chip, j, stage, s):
+    def multiply(chip, j, stage, start):
         first = pl.multiple_of((chip * 2 + core) * rows, rows)
 
         def part(q, carry):
@@ -137,9 +130,9 @@
             dot = functools.partial(jnp.dot, preferred_element_type=jnp.float32)
             mult_re = (dot(left_re, right_re) - dot(left_im, right_im)) * factor
             mult_im = (dot(left_re, right_im) + dot(left_im, right_re)) * factor
-            here = pl.ds(pl.multiple_of(q * step, step), step)
-            stage[s, 0, :, here] = mult_re
-            stage[s, 1, :, here] = mult_im
+            here = pl.ds(pl.multiple_of(start + q * step, step), step)
+            stage[0, :, here] = mult_re
+            stage[1, :, here] = mult_im
             data_re = grid[0, pl.ds(first, rows), pl.ds(column, step)].astype(jnp.float32)
             data_im = grid[1, pl.ds(first, rows), pl.ds(column, step)].astype(jnp.float32)
             for i, term in enumerate((
@@ -158,7 +151,7 @@
 
     acc[...] = jnp.zeros_like(acc)
     mine = grid.at[:, pl.ds(pl.multiple_of(shot * rows, rows), rows), :]
-    load = pltpu.make_async_copy(traces_ref, mine, load_sem)
+    load = pltpu.make_async_copy(traces_ref.at[:, 0], mine, load_sem)
     load.start()
     load.wait()
 
@@ -185,16 +178,9 @@
                 pair(chip, j, slot).start()
             for slot, chip in enumerate((mid, far_mid, far_end, end)):
                 paired(chip, j, slot)
-            s = j % 2
-
-            @pl.when(j >= 2)
-            def _():
-                own_out(j - 2, s).wait()
-            multiply(z, j, own_stage, s)
-            own_out(j, s).start()
+            multiply(z, j, mult_ref, j * width)
 
         loop(0, kept, work)
-        loop(kept - 2, kept, lambda j: own_out(j, j % 2).wait())
 
         def drain(j):
             to_mid(j).wait_send()
@@ -226,14 +212,6 @@
         loop(0, ahead, near)
 
         def work(j):
-            upper = jnp.where(j < kept, jnp.minimum(j + ahead + 1, chunks), chunks)
-            lower = jnp.where(j <= kept, jnp.minimum(j + ahead, chunks), chunks)
-
-            def more(jj):
-                own_sends(jj)
-                near(jj)
-
-            loop(lower, upper, more)
             for slot, chip in ((1, far_mid), (2, far_end)):
                 arrived(chip, j, slot)
 
@@ -241,8 +219,17 @@
                 def _():
                     to_end(chip, j, slot).start()
                 pair(chip, j, slot).start()
-            for slot, chip in enumerate((end, far_mid, far_end, z)):
+            for slot, chip in ((1, far_mid), (2, far_end), (3, z)):
                 paired(chip, j, slot)
+            upper = jnp.where(j < kept, jnp.minimum(j + ahead + 1, chunks), chunks)
+            lower = jnp.where(j <= kept, jnp.minimum(j + ahead, chunks), chunks)
+
+            def more(jj):
+                own_sends(jj)
+                near(jj)
+
+            loop(lower, upper, more)
+            paired(end, j, 0)
             s = j % 2
 
             @pl.when(j >= kept)
@@ -250,14 +237,10 @@
                 @pl.when(j >= kept + 2)
                 def _():
                     result(j - 2, s).wait_send()
-                multiply(end, j, help_stage, s)
+                multiply(end, j, help_stage.at[s], 0)
                 result(j, s).start()
 
-            @pl.when(j >= 2)
-            def _():
-                own_out(j - 2, s).wait()
-            multiply(z, j, own_stage, s)
-            own_out(j, s).start()
+            multiply(z, j, mult_ref, j * width)
 
         loop(0, chunks, work)
 
@@ -296,11 +279,34 @@
     @pl.when(jnp.logical_not(is_end))
     def _():
         def last(j):
-            own_out(j, j % 2).wait()
             result(j, j % 2).wait_send()
         loop(chunks - 2, chunks, last)
 
     loop(1, devices, lambda d: give(d).wait_send())
+
+
+def epilogue_kernel(total_count, total_ref, traces_ref, mult_ref, multiples_ref, primaries_ref, fit):
+    @pl.when(pl.program_id(0) == 0)
+    def _():
+        num_re, num_im, denom = (jnp.sum(total_ref[pl.ds(8 * i, 8), :]) for i in range(3))
+        scaled_den = denom / total_count + epsilon
+        fit[0] = num_re / total_count / scaled_den
+        fit[1] = num_im / total_count / scaled_den
+
+    fit_re = fit[0]
+    fit_im = fit[1]
+    strip = traces_ref.shape[2]
+    first = pl.multiple_of(pl.program_id(0) * strip, strip)
+    mult_re = mult_ref[0, pl.ds(first, strip), :]
+    mult_im = mult_ref[1, pl.ds(first, strip), :]
+    data_re = traces_ref[0, 0].astype(jnp.float32)
+    data_im = traces_ref[1, 0].astype(jnp.float32)
+    prim_re = data_re - (fit_re * mult_re - fit_im * mult_im)
+    prim_im = data_im - (fit_re * mult_im + fit_im * mult_re)
+    multiples_ref[0, 0] = mult_re.astype(jnp.bfloat16)
+    multiples_ref[1, 0] = mult_im.astype(jnp.bfloat16)
+    primaries_ref[0, 0] = prim_re.astype(jnp.bfloat16)
+    primaries_ref[1, 0] = prim_im.astype(jnp.bfloat16)
 
 
 def on_a_line(traces):
@@ -315,30 +321,45 @@
     mult, totals = pl.pallas_call(
         functools.partial(line_kernel, chunks, kept, width, step, freqs, shots),
         out_shape=(
-            jax.ShapeDtypeStruct((2, rows, order), jnp.float32),
+            pltpu.VMEM((2, rows, order), jnp.float32),
             jax.ShapeDtypeStruct((24, 128), jnp.float32),
         ),
-        in_specs=[pl.BlockSpec(memory_space=pl.ANY)],
+        in_specs=[pl.BlockSpec(memory_space=pltpu.HBM)],
         out_specs=(
-            pl.BlockSpec(memory_space=pl.ANY),
+            pl.BlockSpec(memory_space=pltpu.VMEM),
             pl.BlockSpec(memory_space=pltpu.VMEM),
         ),
         scratch_shapes=[
             pltpu.VMEM((2, order, order), jnp.bfloat16),
             pltpu.VMEM((2, 2, rows, width), jnp.float32),
-            pltpu.VMEM((2, 2, rows, width), jnp.float32),
             pltpu.VMEM((24, 128), jnp.float32),
             pltpu.VMEM((devices - 1, 24, 128), jnp.float32),
-            dma, dma((2,)), dma((3, chunks)), dma((4, chunks)), dma((2, chunks)),
+            dma, dma((3, chunks)), dma((4, chunks)), dma((2, chunks)),
             dma((3, chunks)), dma((4, chunks)),
             dma((2,)), dma((chunks,)), dma((devices - 1,)), dma((devices - 1,)),
         ],
         compiler_params=pltpu.CompilerParams(
-            has_side_effects=True, vmem_limit_bytes=60 * 1024 * 1024
+            has_side_effects=True, vmem_limit_bytes=48 * 1024 * 1024
         ),
-    )(traces[:, 0])
-    sums = jnp.sum(totals.reshape(3, 8 * 128), axis=1)
-    return finish(traces, mult[0][None], mult[1][None], sums[0], sums[1], sums[2])
+    )(traces)
+    strip = rows // 12 if rows % (12 * 16) == 0 else rows
+    block = pl.BlockSpec((2, 1, strip, order), lambda i: (0, 0, i, 0))
+    out = jax.ShapeDtypeStruct(traces.shape, traces.dtype)
+    return pl.pallas_call(
+        functools.partial(epilogue_kernel, float(freqs * order * order)),
+        grid=(rows // strip,),
+        out_shape=(out, out),
+        in_specs=[
+            pl.BlockSpec((24, 128), lambda i: (0, 0)),
+            block,
+            pl.BlockSpec(memory_space=pltpu.VMEM),
+        ],
+        out_specs=(block, block),
+        scratch_shapes=[pltpu.SMEM((2,), jnp.float32)],
+        compiler_params=pltpu.CompilerParams(
+            dimension_semantics=("arbitrary",), vmem_limit_bytes=24 * 1024 * 1024
+        ),
+    )(totals, traces, mult)
 
 
 def solution(mesh):

time: 282 us -> 271 us (0.961)
  other arithmetic: 11 us -> 0 us
  Pallas kernels: 265 us -> 270 us
    another operation x2 -> x0, other arithmetic: 10 us -> none  [the longest x1 6.1 us: finish(): primaries = jnp.stack([prim_re, prim_im]).astype(jnp.bfloat16)]
    pallas_call x0 -> x1, Pallas kernels: none -> 7.18 us  [on_a_line(): pl.pallas_call(functools.partial(epilogue_kernel, float(freqs * order * o...]
where the time goes in v2:
time: 271 us
  Pallas kernels  270 us (100%)
    pallas_call x1, Pallas kernels, on_a_line(): pl.pallas_call(functools.partial(line_kernel, chunks, kept, width, step,...  263 us
    pallas_call x1, Pallas kernels, on_a_line(): pl.pallas_call(functools.partial(epilogue_kernel, float(freqs * order * o...  7.18 us

profile of v2, /device:TPU:0, one launch (start us, length us, event | category | flops | bytes accessed | tf_op | source)
XLA Modules:
  0.0 271.1 jit_solution(16265873779322499492)
XLA Ops:
  0.6 0.0 copy-start
  0.6 262.5 %shard_map.30 = (f32[2,384,3072]{2,1,0:T(8,128)S(1)}, f32[24,128]{1,0:T(8,128)}) custom-call(bf16[2,1,384,3072]{3,2,1,0:T(8,128)(2,1)} %traces_ref.3), custom_call_target="tpu_custom_call" | custom-call | tf_op jit(solution)/shard_map/pallas_call | solution.py:321
  263.2 0.0 copy-done
  263.2 0.0 copy-start.1
  263.2 0.7 copy-done.1
  263.9 7.2 %shard_map.31 = (bf16[2,1,384,3072]{3,2,1,0:T(8,128)(2,1)}, bf16[2,1,384,3072]{3,2,1,0:T(8,128)(2,1)}) custom-call(f32[24,128]{1,0:T(8,128)S(1)} %copy-done.1, bf16[2,1,384,3072]{3,2,1,0:T(8,128)(2,1)S(1)} %copy-done, f32[2,384,3072]{2,1,0:T(8,128)S(1)} %get-tuple-element.5.mult_ref), custom_call_target="tpu_custom_call" | custom-call | tf_op jit(solution)/shard_map/pallas_call | solution.py:348
Async XLA Ops:
  0.6 262.6 %copy-start = (bf16[2,1,384,3072]{3,2,1,0:T(8,128)(2,1)S(1)}, bf16[2,1,384,3072]{3,2,1,0:T(8,128)(2,1)}, u32[]{:S(2)}) copy-start(bf16[2,1,384,3072]{3,2,1,0:T(8,128)(2,1)} %traces_ref.3) | copy-start | bytes 14155780
  263.2 0.7 copy-start.1
